TPU v7x, 256 devices: a whole 4x4x8 slice. The times are simulated.
256 devices in a mesh: seq: 16 (over z, core), head: 16 (over x, y).
Axes of the slice: x: 4, y: 4, z: 8, core: 2. Of those that a mesh axis runs over, the one named last changes fastest.
Arguments:
- grad_output: bfloat16 [16384, 4096], P('seq', 'head'), may hold values from -6 to 6
- out_weight: bfloat16 [4096, 8192], P('seq', 'head'), may hold values from -0.0625 to 0.0625
- ssd_out: bfloat16 [16384, 8192], P('seq', 'head'), may hold values from -520 to 520
- gate: bfloat16 [16384, 8192], P('seq', 'head'), may hold values from -5 to 5
- norm_weight: float32 [8192], P('head'), may hold values from 0.5 to 1.5
- time_step: float32 [128, 16384], P('head', 'seq'), may hold values from 0.01 to 0.1
- log_decay: float32 [128, 16384], P('head', 'seq'), may hold values from -0.7 to 0
- state_in: bfloat16 [16384, 8, 128], P('seq'), may hold values from -1.796875 to 1.796875
- state_out: bfloat16 [16384, 8, 128], P('seq'), may hold values from -1.796875 to 1.796875
- skip: float32 [128], P('head'), may hold values from 0.5 to 1.5
Outputs:
- grad_x: bfloat16 [16384, 8192], P('seq', 'head')
- grad_gate: bfloat16 [16384, 8192], P('seq', 'head')
- grad_out_weight: float32 [4096, 8192], P('seq', 'head')
All inputs are finite; a program needn't handle non-finite values.
Results may differ from a plain program's by a relative error of at most 0.014.
Values may be sent and summed in bfloat16 or wider, within the bound.
A program may use at most 128 MiB of HBM per device.

v0:
```python
import math
import jax
import jax.numpy as jnp
from jax import lax
from jax.sharding import Mesh
from jax.sharding import PartitionSpec as P

HEADS = 128
GROUPS = 8
BLOCK_LEN = 256
HEAD = ("head_0", "head_1")
SEQ = ("seq_0", "seq_1")
epsilon = 1e-05


def over_axes(x, axes):
    for axis in axes:
        x = lax.psum(x, axis)
    return x


def nothing_yet(x, identity):
    return jax.tree.map(
        lambda part, zero: jnp.zeros_like(part) + jnp.asarray(zero, part.dtype), x, identity
    )


def carried_in(x, axes, combine, identity):
    before = start = nothing_yet(x, identity)
    running = x
    for axis in reversed(axes):
        size, here = (lax.axis_size(axis), lax.axis_index(axis))
        pieces = jax.tree.map(lambda part: lax.all_gather(part, axis), running)
        inside, running = (start, start)
        for k in reversed(range(size)):
            passed = k > here
            running = combine(running, jax.tree.map(lambda part: part[k], pieces))
            inside = jax.tree.map(lambda new, old: jnp.where(passed, new, old), running, inside)
        before = combine(inside, before)
    return before


def on_device(
    grad_output,
    out_weight,
    ssd_out,
    gate,
    norm_weight,
    time_step,
    log_decay,
    state_in,
    state_out,
    skip,
):
    tok_rows = ssd_out.shape[0]
    local_width = ssd_out.shape[1]
    total_width = local_width * lax.axis_size(HEAD)
    full_grad = lax.all_gather(grad_output, HEAD, axis=1, tiled=True)
    values = ssd_out.astype(jnp.float32)
    gate_values = gate.astype(jnp.float32)
    sigmoid_gate = jax.nn.sigmoid(gate_values)
    silu_gate = gate_values * sigmoid_gate
    gated_values = values * silu_gate
    local_squares = jnp.sum(gated_values * gated_values, axis=1)
    columns = full_grad
    normed_grad = jnp.dot(
        columns,
        lax.all_gather(out_weight, SEQ, axis=0, tiled=True),
        preferred_element_type=jnp.float32,
    )
    squares = over_axes(local_squares, HEAD)
    weighted = over_axes(jnp.sum(norm_weight * normed_grad * gated_values, axis=1), HEAD)
    inverse_rms = lax.rsqrt(squares[:, None] / total_width + epsilon)
    normed = (gated_values * inverse_rms * norm_weight).astype(jnp.bfloat16)
    gated_grad = (
        inverse_rms * norm_weight * normed_grad
        - gated_values * inverse_rms**3 * weighted[:, None] / total_width
    )
    grad_gate = (
        gated_grad * values * sigmoid_gate * (1.0 + gate_values * (1.0 - sigmoid_gate))
    ).astype(jnp.bfloat16)
    grad_ssd = (gated_grad * silu_gate).astype(jnp.bfloat16)
    columns = full_grad
    weight_sum = lax.psum_scatter(
        lax.dot_general(
            columns, normed, (((0,), (0,)), ((), ())), preferred_element_type=jnp.float32
        ).astype(jnp.bfloat16),
        SEQ,
        scatter_dimension=0,
        tiled=True,
    ).astype(jnp.float32)
    grad_out_weight = weight_sum * (1.0 / math.sqrt(tok_rows * lax.axis_size(SEQ)))
    heads_here = time_step.shape[0]
    head_width = local_width // heads_here
    blocks = tok_rows // BLOCK_LEN
    state_width = state_in.shape[2]
    group_count = state_in.shape[1]
    first_head = lax.axis_index(HEAD) * heads_here
    head_ids = first_head + jnp.arange(heads_here, dtype=jnp.int32)
    group_ids = head_ids // (HEADS // GROUPS)
    group_pick = (group_ids[:, None] == jnp.arange(group_count, dtype=jnp.int32)[None, :]).astype(
        jnp.bfloat16
    )
    b_heads = jnp.einsum(
        "tgn,hg->htn", state_in, group_pick, preferred_element_type=jnp.float32
    ).astype(jnp.bfloat16)
    b_heads = b_heads.reshape(heads_here, blocks, BLOCK_LEN, state_width)
    c_heads = jnp.einsum(
        "tgn,hg->htn", state_out, group_pick, preferred_element_type=jnp.float32
    ).astype(jnp.bfloat16)
    c_heads = c_heads.reshape(heads_here, blocks, BLOCK_LEN, state_width)
    grad_heads = grad_ssd.reshape(tok_rows, heads_here, head_width).transpose(1, 0, 2)
    grad_heads = grad_heads.reshape(heads_here, blocks, BLOCK_LEN, head_width)
    cumulative = jnp.cumsum(log_decay.reshape(heads_here, blocks, BLOCK_LEN), axis=2)
    block_total = cumulative[..., -1]
    sequence_indices = jnp.arange(BLOCK_LEN)
    upper_mask = sequence_indices[None, :] >= sequence_indices[:, None]
    scores = jnp.einsum("hktn,hksn->hkts", b_heads, c_heads, preferred_element_type=jnp.float32)
    log_gap = cumulative[..., None, :] - cumulative[..., :, None]
    block_weights = jnp.where(upper_mask, scores * jnp.exp(jnp.minimum(log_gap, 0.0)), 0.0).astype(
        jnp.bfloat16
    )
    within = jnp.einsum(
        "hkts,hksp->hktp", block_weights, grad_heads, preferred_element_type=jnp.float32
    )
    grad_float = grad_heads.astype(jnp.float32)
    scaled = (jnp.exp(cumulative)[..., None] * grad_float).astype(jnp.bfloat16)
    block_state = jnp.einsum("hksp,hksn->hkpn", scaled, c_heads, preferred_element_type=jnp.float32)

    def fold_block(carried, inputs):
        state_now, total_now = inputs
        return (state_now + jnp.exp(total_now)[:, None, None] * carried, carried)

    zero_state = jnp.zeros((heads_here, head_width, state_width), jnp.float32)
    summary, inside = lax.scan(
        fold_block, zero_state, (block_state.transpose(1, 0, 2, 3), block_total.T), reverse=True
    )
    decay_total = jnp.exp(jnp.sum(block_total, axis=1))
    tail_decay = jnp.exp(
        jnp.sum(block_total, axis=1, keepdims=True) - jnp.cumsum(block_total, axis=1)
    )

    def combine_pair(earlier, later):
        return (later[0] * earlier[0], later[1] + later[0][:, None, None] * earlier[1])

    identity = (jnp.ones((heads_here,), jnp.float32), zero_state)
    prefix = carried_in((decay_total, summary), SEQ, combine_pair, identity)
    remote = prefix[1]
    full_states = inside.transpose(1, 0, 2, 3) + tail_decay[..., None, None] * remote[:, None]
    carry_low = full_states.astype(jnp.bfloat16)
    across = jnp.einsum("hkpn,hktn->hktp", carry_low, b_heads, preferred_element_type=jnp.float32)
    across = across * jnp.exp(block_total[..., None] - cumulative)[..., None]
    step_sizes = time_step.reshape(heads_here, blocks, BLOCK_LEN)
    grad_head = step_sizes[..., None] * (within + across) + skip[:, None, None, None] * grad_float
    grad_x = (
        grad_head.reshape(heads_here, tok_rows, head_width)
        .transpose(1, 0, 2)
        .reshape(tok_rows, local_width)
    )
    return (grad_x.astype(jnp.bfloat16), grad_gate, grad_out_weight)


def solution(mesh):
    finer = Mesh(mesh.devices.reshape(8, 2, 4, 4), ("seq_0", "seq_1", "head_0", "head_1"))
    return jax.shard_map(
        on_device,
        mesh=finer,
        in_specs=(
            P(SEQ, HEAD),
            P(SEQ, HEAD),
            P(SEQ, HEAD),
            P(SEQ, HEAD),
            P(HEAD),
            P(HEAD, SEQ),
            P(HEAD, SEQ),
            P(SEQ, None, None),
            P(SEQ, None, None),
            P(HEAD),
        ),
        out_specs=(P(SEQ, HEAD), P(SEQ, HEAD), P(SEQ, HEAD)),
        check_vma=False,
    )
```

profile of v0, /device:TPU:2, one launch (start us, length us, event | category | flops | bytes accessed | tf_op | source)
XLA Modules:
  0.0 294.2 jit_solution(11251501523468864543)
XLA Ops:
  8.7 1.3 dynamic-slice.1
  13.3 2.3 reduce-window.6
  16.2 1.5 copy.74
  17.7 2.6 copy.75
  20.4 2.4 all-reduce
  23.1 2.1 convolution_convert_fusion.1
  25.2 29.5 %all-gather.9.cloned.1.call-done = bf16[4096,512]{1,0:T(8,128)(2,1)} async-done(((bf16[256,512]{1,0:T(8,128)(2,1)}), bf16[4096,512]{1,0:T(8,128)(2,1)}) %all-gather.9.cloned.1.call-update) | async-done | bytes 4194320 | tf_op jit(solution)/shard_map/all_gather | solution.py:68
  54.7 82.9 %all-gather.7.cloned.1.call-done = bf16[1024,4096]{1,0:T(8,128)(2,1)} async-done(((bf16[1024,256]{1,0:T(8,128)(2,1)}), bf16[1024,4096]{1,0:T(8,128)(2,1)}) %all-gather.7.cloned.1.call-update) | async-done | bytes 8388624 | tf_op jit(solution)/shard_map/all_gather | solution.py:58
  137.6 11.3 %multiply_reduce_fusion.1 = (f32[1024]{0:T(1024)S(1)}, f32[1024]{0:T(1024)S(1)}, f32[1024,512]{0,1:T(8,128)}) fusion(bf16[1024,512]{0,1:T(8,128)(2,1)S(1)} %copy.74, bf16[1024,512]{0,1:T(8,128)(2,1)} %copy.75, f32[512]{0:T(512)S(1)} %copy-done.7, bf16[1024,4096]{1,0:T(8,128)(2,1)} %all-gather.7.cloned.1.call-done, ...), kind=kOutput, calls=%fused_computation.32 | convolution fusion | flops 4301256704 | bytes 16787456 | tf_op jit(solution)/shard_map/dot_general | solution.py:66
  148.8 8.7 %all-reduce.3 = (f32[1024]{0:T(1024)S(1)}, f32[1024]{0:T(1024)S(1)}) all-reduce(f32[1024]{0:T(1024)S(1)} %get-tuple-element.160, f32[1024]{0:T(1024)S(1)} %get-tuple-element.159), channel_id=1, replica_groups=mesh['seq_0'=8,'seq_1'=2,'head_0'=4,'head_1'=4] {'head_0'}, use_global_device_ids=true, to_apply=%region_6.0 | all-reduce | flops 2048 | bytes 16384 | tf_op jit(solution)/shard_map/psum | solution.py:18
  157.5 10.2 %all-reduce.2 = (f32[1024]{0:T(1024)S(1)}, f32[1024]{0:T(1024)S(1)}) all-reduce(f32[1024]{0:T(1024)S(1)} %get-tuple-element.175, f32[1024]{0:T(1024)S(1)} %get-tuple-element.176), channel_id=1, replica_groups=mesh['seq_0'=8,'seq_1'=2,'head_0'=4,'head_1'=4] {'head_1'}, use_global_device_ids=true, to_apply=%region_7.8 | all-reduce | flops 2048 | bytes 16384 | tf_op jit(solution)/shard_map/psum | solution.py:18
  167.8 4.7 %fusion.9 = (bf16[1024,512]{0,1:T(8,128)(2,1)}, bf16[1024,512]{0,1:T(8,128)(2,1)S(1)}) fusion(bf16[1024,512]{0,1:T(8,128)(2,1)S(1)} %copy.74, bf16[1024,512]{0,1:T(8,128)(2,1)} %copy.75, f32[1024]{0:T(1024)S(1)} %get-tuple-element.173, f32[1024]{0:T(1024)S(1)} %get-tuple-element.182, f32[1024,512]{0,1:T(8,128)} %get-tuple-element.195, f32[512]{0:T(512)S(1)} %copy-done.7, ...), kind=kLoop, calls=%fused_computation.20 | loop fusion | flops 11534336 | bytes 6305792 | tf_op jit(solution)/shard_map/convert_element_type | solution.py:81
  172.5 1.8 fusion.27
  174.3 4.5 %while.17 = (s32[]{:T(128)}, f32[8,64,128]{2,1,0:T(8,128)S(1)}, f32[4,8,64,128]{3,2,1,0:T(8,128)S(1)}, f32[4,8,64,128]{3,2,0,1:T(8,128)}, f32[4,8]{1,0:T(4,128)S(1)}, /*index=5*/s32[]{:T(128)}, s32[]{:T(128)}, s32[]{:T(128)}) while((s32[]{:T(128)}, f32[8,64,128]{2,1,0:T(8,128)S(1)}, f32[4,8,64,128]{3,2,1,0:T(8,128)S(1)}, ...), condition=%wide.region_9.10_spmd.clone, body=%wide.region_8.9_spmd.clone.sunk | while | flops 262148 | bytes 1310944 | solution.py:135
  179.8 2.2 all-gather
  183.0 11.0 %fusion.2 = bf16[4096,512]{0,1:T(8,128)(2,1)} fusion(bf16[1024,4096]{1,0:T(8,128)(2,1)} %all-gather.7.cloned.1.call-done, f32[512]{0:T(512)S(1)} %copy-done.7, bf16[1024,512]{0,1:T(8,128)(2,1)} %copy-done.2, f32[1024]{0:T(1024)S(1)} %get-tuple-element.181, bf16[1024,512]{0,1:T(8,128)(2,1)} %copy.75), kind=kOutput, calls=%fused_computation.7 | convolution fusion | flops 4302307328 | bytes 14686208 | tf_op jit(solution)/shard_map/dot_general | solution.py:85
  194.9 17.7 %all-reduce.1 = f32[64]{0:T(128)S(1)} all-reduce(f32[64]{0:T(128)S(1)} %copy-done.10), channel_id=4, replica_groups=mesh['seq_0'=8,'seq_1'=2,'head_0'=4,'head_1'=4] {'seq_0'}, use_global_device_ids=true, to_apply=%add.1 | all-reduce | flops 64 | bytes 512
  212.7 3.7 %convolution_convert_fusion.2 = bf16[8,1024,128]{2,0,1:T(8,128)(2,1)} fusion(bf16[1024,8,128]{2,1,0:T(8,128)(2,1)} %param.19, s32[8]{0:T(128)S(1)} %and_select_fusion), kind=kOutput, calls=%fused_computation.34 | convolution fusion | flops 17825856 | bytes 4194336 | tf_op jit(solution)/shard_map/tgn,hg->htn/dot_general | solution.py:104
  216.3 2.3 copy.86
  218.6 6.3 %fusion.3 = f32[8,4,256,64]{2,3,1,0:T(8,128)} fusion(f32[8,4,256]{2,1,0:T(4,128)S(1)} %copy.72, pred[256,256]{1,0:T(8,128)(4,1)S(1)} %iota_compare_fusion, bf16[8,4,256,128]{3,0,2,1:T(8,128)(2,1)} %bitcast.136, bf16[8,4,256,128]{3,0,2,1:T(8,128)(2,1)} %bitcast.130, bf16[8,8,4,8,256]{4,3,2,1,0:T(8,128)(2,1)} %bitcast.133), kind=kOutput, calls=%fused_computation.8 | convolution fusion | flops 815792128 | bytes 7438336 | tf_op jit(solution)/shard_map/hkts,hksp->hktp/dot_general | solution.py:123
  224.9 2.1 fusion.53
  227.2 3.3 %fusion.30 = bf16[8,4,8,8,256]{4,3,2,1,0:T(8,128)(2,1)S(1)} fusion(f32[8,4,256,64]{2,3,1,0:T(8,128)} %fusion.3, bf16[8,4,256,128]{3,0,2,1:T(8,128)(2,1)S(1)} %bitcast.131, f32[8]{0:T(128)S(1)} %copy-done.8, f32[8,4,256]{2,1,0:T(4,128)S(1)} %copy.83, f32[8,4,256]{2,1,0:T(4,128)S(1)} %copy.67, bf16[8,8,4,8,256]{4,3,2,1,0:T(8,128)(2,1)} %bitcast.134, ...), kind=kOutput, calls=%fused_computation.42 | convolution fusion | flops 138674176 | bytes 7667872 | tf_op jit(solution)/shard_map/hkpn,hktn->hktp/dot_general | solution.py:151
  230.6 1.3 copy.85
  231.9 53.7 %reduce-scatter.2.cloned.1.call-done = bf16[256,512]{0,1:T(8,128)(2,1)} async-done(((bf16[4096,512]{0,1:T(8,128)(2,1)}), bf16[256,512]{0,1:T(8,128)(2,1)}) %reduce-scatter.2.cloned.1.call-update) | async-done | bytes 262160 | tf_op jit(solution)/shard_map/reduce_scatter | solution.py:84
  (71 shorter events, 14.0 us)
Async XLA Ops:
  7.2 15.9 %copy-start = (bf16[1024,8,128]{2,1,0:T(8,128)(2,1)S(1)}, bf16[1024,8,128]{2,1,0:T(8,128)(2,1)}, u32[]{:S(2)}) copy-start(bf16[1024,8,128]{2,1,0:T(8,128)(2,1)} %param.20) | copy-start | bytes 6291460
  7.2 47.5 %all-gather.9.cloned.1.call-start = ((), (), s32[]{:S(2)}) async-start(), calls=%async_computation.2 | async-start | bytes 4456448 | tf_op jit(solution)/shard_map/all_gather | solution.py:68
  7.9 129.7 %all-gather.7.cloned.1.call-start = ((), (), s32[]{:S(2)}) async-start(), calls=%async_computation.1 | async-start | bytes 8912896 | tf_op jit(solution)/shard_map/all_gather | solution.py:58
  8.7 216.3 %all-gather.11.cloned.1.call-start = ((), (), s32[]{:S(2)}) async-start(), calls=%async_computation.3 | async-start | bytes 2359296 | tf_op jit(solution)/shard_map/all_gather | solution.py:33
  17.7 150.1 %copy-start.2 = (bf16[1024,512]{0,1:T(8,128)(2,1)}, bf16[1024,512]{0,1:T(8,128)(2,1)S(1)}, u32[]{:S(2)}) copy-start(bf16[1024,512]{0,1:T(8,128)(2,1)S(1)} %copy.74) | copy-start | bytes 3145732
  23.1 2.1 copy-start.9
  23.1 114.5 %copy-start.7 = (f32[512]{0:T(512)S(1)}, f32[512]{0:T(512)}, u32[]{:S(2)}) copy-start(f32[512]{0:T(512)} %param.16) | copy-start | bytes 6148
  167.8 4.7 %copy-start.5 = (bf16[8,1024,128]{2,0,1:T(8,128)(2,1)S(1)}, bf16[8,1024,128]{2,0,1:T(8,128)(2,1)}, u32[]{:S(2)}) copy-start(bf16[8,1024,128]{2,0,1:T(8,128)(2,1)} %convolution_convert_fusion.1) | copy-start | bytes 6291460
  172.5 1.8 copy-start.3
  178.8 1.0 copy-start.4
  182.8 102.8 %reduce-scatter.2.cloned.1.call-start = ((), (), s32[]{:S(2)}) async-start(), calls=%async_computation.4 | async-start | bytes 4456448 | tf_op jit(solution)/shard_map/reduce_scatter | solution.py:84
  194.0 0.8 copy-start.6
  194.1 0.8 copy-start.10
  224.9 2.1 copy-start.8
  224.9 2.2 copy-start.1
Sparse Core Ops, SparseCore 0:
  9.8 44.8 all-gather.8
  57.1 80.4 all-gather.6
  182.9 38.5 all-gather.10
  223.9 61.6 reduce-scatter.1
where the time goes:
time: 295 us; the launch traced here: 294 us
  waiting for transfers between devices  167 us (57%)
  blocking collectives  41.2 us (14%)
  matrix products  39.5 us (13%)
  other arithmetic  15.8 us (5%)
  between operations  15.3 us (5%)
  local copies, waits for them, and re-layouts  14.4 us (5%)
    all_gather x1, waiting for transfers between devices, on_device(): full_grad = lax.all_gather(grad_output, HEAD, axis=1, tiled=True)  82.9 us
    reduce_scatter x1, waiting for transfers between devices, on_device(): lax.psum_scatter(lax.dot_general(columns, normed, (((0,), (0,)), ((), ())...  53.7 us
    all_gather x1, waiting for transfers between devices, on_device(): lax.all_gather(out_weight, SEQ, axis=0, tiled=True)  29.5 us
    unnamed x2, blocking collectives  20.1 us
    psum x2, blocking collectives, over_axes(): x = lax.psum(x, axis)  18.9 us
    unnamed x32, local copies, waits for them, and re-layouts  13.2 us
    dot_general x1, matrix products, on_device(): jnp.dot(columns, lax.all_gather(out_weight, SEQ, axis=0, tiled=True), pre...  11.3 us
    dot_general x1, matrix products, on_device(): lax.dot_general(columns, normed, (((0,), (0,)), ((), ())), preferred_elem...  11 us
  transfers between devices with their start and end apart: 4, of which 3 were waited for; matrix products, arithmetic and copies ran while one was open for 15% of the time, Pallas kernels for 0%

commit v1 on v0

--- a/solution.py
+++ b/solution.py
@@ -65,7 +65,9 @@
     columns = full_grad
     normed_grad = jnp.dot(
         columns,
-        lax.all_gather(out_weight, SEQ, axis=0, tiled=True),
+        jnp.concatenate(
+            lax.all_to_all(jnp.stack([out_weight] * lax.axis_size(SEQ)), SEQ, 0, 0), axis=0
+        ),
         preferred_element_type=jnp.float32,
     )
     squares = over_axes(local_squares, HEAD)

time: 295 us -> 271 us (0.919)
  waiting for transfers between devices: 167 us -> 135 us
  starting transfers between devices: 0.34 us -> 8.92 us
    all_gather x1, waiting for transfers between devices: 82.9 us -> 0.01 us  [on_device(): full_grad = lax.all_gather(grad_output, HEAD, axis=1, tiled=True)]
    all_to_all x0 -> x1, waiting for transfers between devices: none -> 79.8 us  [on_device(): lax.all_to_all(jnp.stack([out_weight] * lax.axis_size(SEQ)), SEQ, 0, 0)]
    all_gather x1 -> x0, waiting for transfers between devices: 29.5 us -> none  [on_device(): lax.all_gather(out_weight, SEQ, axis=0, tiled=True)]
    all_to_all x0 -> x1, starting transfers between devices: none -> 8.62 us  [on_device(): lax.all_to_all(jnp.stack([out_weight] * lax.axis_size(SEQ)), SEQ, 0, 0)]
    another operation x2 -> x3, local copies, waits for them, and re-layouts: 0.02 us -> 3.31 us  [the longest x1 3.29 us: on_device(): jnp.stack([out_weight] * lax.axis_size(SEQ))]
    unnamed x32 -> x38, local copies, waits for them, and re-layouts: 13.2 us -> 11.9 us
  transfers between devices with their start and end apart: 4 -> 4, of which waited for: 3 -> 2; matrix products, arithmetic and copies ran while one was open for 15% -> 16% of each run, Pallas kernels for 0% -> 0%
where the time goes in v1:
time: 271 us; the launch traced here: 270 us
  waiting for transfers between devices  135 us (50%)
  blocking collectives  39.9 us (15%)
  matrix products  39.5 us (15%)
  other arithmetic  15.8 us (6%)
  local copies, waits for them, and re-layouts  15.7 us (6%)
  between operations  15.3 us (6%)
  starting transfers between devices  8.92 us (3%)
    all_to_all x1, waiting for transfers between devices, on_device(): lax.all_to_all(jnp.stack([out_weight] * lax.axis_size(SEQ)), SEQ, 0, 0)  79.8 us
    reduce_scatter x1, waiting for transfers between devices, on_device(): lax.psum_scatter(lax.dot_general(columns, normed, (((0,), (0,)), ((), ())...  54.7 us
    psum x2, blocking collectives, over_axes(): x = lax.psum(x, axis)  19.6 us
    unnamed x2, blocking collectives  18.2 us
    unnamed x38, local copies, waits for them, and re-layouts  11.9 us
    dot_general x1, matrix products, on_device(): jnp.dot(columns, jnp.concatenate(lax.all_to_all(jnp.stack([out_weight] *...  11.3 us
    dot_general x1, matrix products, on_device(): lax.dot_general(columns, normed, (((0,), (0,)), ((), ())), preferred_elem...  11 us
    all_to_all x1, starting transfers between devices, on_device(): lax.all_to_all(jnp.stack([out_weight] * lax.axis_size(SEQ)), SEQ, 0, 0)  8.62 us
  transfers between devices with their start and end apart: 4, of which 2 were waited for; matrix products, arithmetic and copies ran while one was open for 16% of the time, Pallas kernels for 0%

profile of v1, /device:TPU:2, one launch (start us, length us, event | category | flops | bytes accessed | tf_op | source)
XLA Modules:
  0.0 270.5 jit_solution(18068990527524542839)
XLA Ops:
  7.9 3.3 %stack.2 = bf16[16,256,512]{2,1,0:T(8,128)(2,1)} broadcast(bf16[256,512]{1,0:T(8,128)(2,1)} %param.13), dimensions={1,2} | broadcast | bytes 4456448 | tf_op jit(solution)/shard_map/stack | solution.py:69
  11.2 8.6 %all-to-all-start = ((bf16[16,256,512]{2,1,0:T(8,128)(2,1)}), bf16[16,256,512]{2,1,0:T(8,128)(2,1)}, u32[]{:S(2)}, u32[]{:S(2)}) async-start(bf16[16,256,512]{2,1,0:T(8,128)(2,1)} %stack.2), calls=%async_computation | async-start | bytes 8388608 | tf_op jit(solution)/shard_map/all_to_all | solution.py:69
  19.9 1.5 copy.74
  21.5 2.6 copy.75
  24.1 2.3 reduce-window.6
  29.6 2.5 all-reduce
  32.3 2.1 convolution_convert_fusion.1
  34.4 79.8 %all-to-all-done = bf16[16,256,512]{2,1,0:T(8,128)(2,1)} async-done(((bf16[16,256,512]{2,1,0:T(8,128)(2,1)}), bf16[16,256,512]{2,1,0:T(8,128)(2,1)}, u32[]{:S(2)}, u32[]{:S(2)}) %all-to-all-start) | async-done | bytes 4194336 | tf_op jit(solution)/shard_map/all_to_all | solution.py:69
  114.2 11.3 %multiply_reduce_fusion.1 = (f32[1024]{0:T(1024)S(1)}, f32[1024]{0:T(1024)S(1)}, f32[1024,512]{0,1:T(8,128)}) fusion(bf16[1024,512]{0,1:T(8,128)(2,1)S(1)} %copy.74, bf16[1024,512]{0,1:T(8,128)(2,1)} %copy.75, f32[512]{0:T(512)S(1)} %copy-done.8, bf16[1024,4096]{1,0:T(8,128)(2,1)} %all-gather.6.cloned.1.call-done, bf16[4096,512]{1,0:T(8,128)(2,1)} %bitcast.5), kind=kOutput, calls=%fused_computation.32 | convolution fusion | flops 4301256704 | bytes 16787456 | tf_op jit(solution)/shard_map/dot_general | solution.py:66
  125.5 8.7 %all-reduce.3 = (f32[1024]{0:T(1024)S(1)}, f32[1024]{0:T(1024)S(1)}) all-reduce(f32[1024]{0:T(1024)S(1)} %get-tuple-element.160, f32[1024]{0:T(1024)S(1)} %get-tuple-element.159), channel_id=1, replica_groups=mesh['seq_0'=8,'seq_1'=2,'head_0'=4,'head_1'=4] {'head_0'}, use_global_device_ids=true, to_apply=%region_6.0 | all-reduce | flops 2048 | bytes 16384 | tf_op jit(solution)/shard_map/psum | solution.py:18
  134.2 10.9 %all-reduce.2 = (f32[1024]{0:T(1024)S(1)}, f32[1024]{0:T(1024)S(1)}) all-reduce(f32[1024]{0:T(1024)S(1)} %get-tuple-element.175, f32[1024]{0:T(1024)S(1)} %get-tuple-element.176), channel_id=1, replica_groups=mesh['seq_0'=8,'seq_1'=2,'head_0'=4,'head_1'=4] {'head_1'}, use_global_device_ids=true, to_apply=%region_7.8 | all-reduce | flops 2048 | bytes 16384 | tf_op jit(solution)/shard_map/psum | solution.py:18
  145.1 4.7 %fusion.9 = (bf16[1024,512]{0,1:T(8,128)(2,1)}, bf16[1024,512]{0,1:T(8,128)(2,1)S(1)}) fusion(bf16[1024,512]{0,1:T(8,128)(2,1)S(1)} %copy.74, bf16[1024,512]{0,1:T(8,128)(2,1)} %copy.75, f32[1024]{0:T(1024)S(1)} %get-tuple-element.173, f32[1024]{0:T(1024)S(1)} %get-tuple-element.182, f32[1024,512]{0,1:T(8,128)} %get-tuple-element.195, f32[512]{0:T(512)S(1)} %copy-done.8, ...), kind=kLoop, calls=%fused_computation.20 | loop fusion | flops 11534336 | bytes 6305792 | tf_op jit(solution)/shard_map/convert_element_type | solution.py:83
  149.7 1.8 fusion.27
  151.7 4.5 %while.17 = (s32[]{:T(128)}, f32[8,64,128]{2,1,0:T(8,128)S(1)}, f32[4,8,64,128]{3,2,1,0:T(8,128)S(1)}, f32[4,8,64,128]{3,2,0,1:T(8,128)}, f32[4,8]{1,0:T(4,128)S(1)}, /*index=5*/s32[]{:T(128)}, s32[]{:T(128)}, s32[]{:T(128)}) while((s32[]{:T(128)}, f32[8,64,128]{2,1,0:T(8,128)S(1)}, f32[4,8,64,128]{3,2,1,0:T(8,128)S(1)}, ...), condition=%wide.region_9.10_spmd.clone, body=%wide.region_8.9_spmd.clone.sunk | while | flops 262148 | bytes 1310936 | solution.py:137
  157.2 2.2 all-gather
  160.4 11.0 %fusion.2 = bf16[4096,512]{0,1:T(8,128)(2,1)} fusion(bf16[1024,4096]{1,0:T(8,128)(2,1)} %all-gather.6.cloned.1.call-done, f32[512]{0:T(512)S(1)} %copy-done.8, bf16[1024,512]{0,1:T(8,128)(2,1)} %copy-done.2, f32[1024]{0:T(1024)S(1)} %get-tuple-element.181, bf16[1024,512]{0,1:T(8,128)(2,1)} %copy.75), kind=kOutput, calls=%fused_computation.7 | convolution fusion | flops 4302307328 | bytes 14686208 | tf_op jit(solution)/shard_map/dot_general | solution.py:87
  172.2 15.7 %all-reduce.1 = f32[64]{0:T(128)S(1)} all-reduce(f32[64]{0:T(128)S(1)} %copy-done.11), channel_id=4, replica_groups=mesh['seq_0'=8,'seq_1'=2,'head_0'=4,'head_1'=4] {'seq_0'}, use_global_device_ids=true, to_apply=%add.1 | all-reduce | flops 64 | bytes 512
  188.0 3.7 %convolution_convert_fusion.2 = bf16[8,1024,128]{2,0,1:T(8,128)(2,1)} fusion(bf16[1024,8,128]{2,1,0:T(8,128)(2,1)} %param.19, s32[8]{0:T(128)S(1)} %and_select_fusion), kind=kOutput, calls=%fused_computation.34 | convolution fusion | flops 17825856 | bytes 4194336 | tf_op jit(solution)/shard_map/tgn,hg->htn/dot_general | solution.py:106
  191.6 2.3 copy.86
  193.9 6.4 %fusion.3 = f32[8,4,256,64]{2,3,1,0:T(8,128)} fusion(f32[8,4,256]{2,1,0:T(4,128)S(1)} %copy.72, pred[256,256]{1,0:T(8,128)(4,1)S(1)} %iota_compare_fusion, bf16[8,4,256,128]{3,0,2,1:T(8,128)(2,1)} %bitcast.137, bf16[8,4,256,128]{3,0,2,1:T(8,128)(2,1)} %bitcast.131, bf16[8,8,4,8,256]{4,3,2,1,0:T(8,128)(2,1)} %bitcast.134), kind=kOutput, calls=%fused_computation.8 | convolution fusion | flops 815792128 | bytes 7438336 | tf_op jit(solution)/shard_map/hkts,hksp->hktp/dot_general | solution.py:125
  200.3 2.1 fusion.53
  202.5 3.3 %fusion.30 = bf16[8,4,8,8,256]{4,3,2,1,0:T(8,128)(2,1)S(1)} fusion(f32[8,4,256,64]{2,3,1,0:T(8,128)} %fusion.3, bf16[8,4,256,128]{3,0,2,1:T(8,128)(2,1)S(1)} %bitcast.132, f32[8]{0:T(128)S(1)} %copy-done.9, f32[8,4,256]{2,1,0:T(4,128)S(1)} %copy.83, f32[8,4,256]{2,1,0:T(4,128)S(1)} %copy.67, bf16[8,8,4,8,256]{4,3,2,1,0:T(8,128)(2,1)} %bitcast.135, ...), kind=kOutput, calls=%fused_computation.42 | convolution fusion | flops 138674176 | bytes 7667872 | tf_op jit(solution)/shard_map/hkpn,hktn->hktp/dot_general | solution.py:153
  206.0 1.3 copy.85
  207.3 54.7 %reduce-scatter.2.cloned.1.call-done = bf16[256,512]{0,1:T(8,128)(2,1)} async-done(((bf16[4096,512]{0,1:T(8,128)(2,1)}), bf16[256,512]{0,1:T(8,128)(2,1)}) %reduce-scatter.2.cloned.1.call-update) | async-done | bytes 262160 | tf_op jit(solution)/shard_map/reduce_scatter | solution.py:86
  (77 shorter events, 12.5 us)
Async XLA Ops:
  7.2 25.1 %copy-start = (bf16[1024,8,128]{2,1,0:T(8,128)(2,1)S(1)}, bf16[1024,8,128]{2,1,0:T(8,128)(2,1)}, u32[]{:S(2)}) copy-start(bf16[1024,8,128]{2,1,0:T(8,128)(2,1)} %param.20) | copy-start | bytes 6291460
  7.2 107.0 %all-gather.6.cloned.1.call-start = ((), (), s32[]{:S(2)}) async-start(), calls=%async_computation.2 | async-start | bytes 8912896 | tf_op jit(solution)/shard_map/all_gather | solution.py:58
  11.2 103.0 %all-to-all-start = ((bf16[16,256,512]{2,1,0:T(8,128)(2,1)}), bf16[16,256,512]{2,1,0:T(8,128)(2,1)}, u32[]{:S(2)}, u32[]{:S(2)}) async-start(bf16[16,256,512]{2,1,0:T(8,128)(2,1)} %stack.2), calls=%async_computation | async-start | bytes 8388608 | tf_op jit(solution)/shard_map/all_to_all | solution.py:69
  19.8 180.4 %all-gather.8.cloned.1.call-start = ((), (), s32[]{:S(2)}) async-start(), calls=%async_computation.3 | async-start | bytes 2359296 | tf_op jit(solution)/shard_map/all_gather | solution.py:33
  19.9 4.2 %copy-start.6 = (f32[8,1024]{1,0:T(8,128)S(1)}, f32[8,1024]{1,0:T(8,128)}, u32[]{:S(2)}) copy-start(f32[8,1024]{1,0:T(8,128)} %param.18) | copy-start | bytes 98308
  19.9 7.1 %copy-start.13 = (u32[256]{0:T(256)S(1)}, u32[256]{0:T(256)}, u32[]{:S(2)}) copy-start(u32[256]{0:T(256)} %constant.117) | copy-start | bytes 3076
  19.9 7.7 %copy-start.12 = (u32[256]{0:T(256)S(1)}, u32[256]{0:T(256)}, u32[]{:S(2)}) copy-start(u32[256]{0:T(256)} %constant.122) | copy-start | bytes 3076
  21.4 123.6 %copy-start.2 = (bf16[1024,512]{0,1:T(8,128)(2,1)}, bf16[1024,512]{0,1:T(8,128)(2,1)S(1)}, u32[]{:S(2)}) copy-start(bf16[1024,512]{0,1:T(8,128)(2,1)S(1)} %copy.74) | copy-start | bytes 3145732
  32.3 2.1 copy-start.10
  32.3 81.9 %copy-start.8 = (f32[512]{0:T(512)S(1)}, f32[512]{0:T(512)}, u32[]{:S(2)}) copy-start(f32[512]{0:T(512)} %param.16) | copy-start | bytes 6148
  145.1 4.7 %copy-start.5 = (bf16[8,1024,128]{2,0,1:T(8,128)(2,1)S(1)}, bf16[8,1024,128]{2,0,1:T(8,128)(2,1)}, u32[]{:S(2)}) copy-start(bf16[8,1024,128]{2,0,1:T(8,128)(2,1)} %convolution_convert_fusion.1) | copy-start | bytes 6291460
  149.7 1.8 copy-start.3
  156.2 1.0 copy-start.4
  160.2 101.8 %reduce-scatter.2.cloned.1.call-start = ((), (), s32[]{:S(2)}) async-start(), calls=%async_computation.4 | async-start | bytes 4456448 | tf_op jit(solution)/shard_map/reduce_scatter | solution.py:86
  171.4 0.8 copy-start.7
  171.4 0.8 copy-start.11
  200.3 2.1 copy-start.9
  200.3 2.2 copy-start.1
Sparse Core Ops, SparseCore 0:
  10.4 84.9 all-gather.5
  160.3 37.3 all-gather.7
  200.2 61.6 reduce-scatter.1
